TPU v7x, 32 devices: a whole 2x2x4 slice. The times are simulated.
32 devices in a mesh: replica: 4 (over x, core), fsdp: 8 (over z, y).
Axes of the slice: x: 2, y: 2, z: 4, core: 2. Of those that a mesh axis runs over, the one named last changes fastest.
Arguments:
- deltas: bfloat16 [4, 2, 2048, 16384], P('replica', None, 'fsdp'), may hold values from -3 to 3
- master: float32 [2, 2048, 16384], P(None, 'replica', 'fsdp'), may hold values from -3 to 3
- momentum: float32 [2, 2048, 16384], P(None, 'replica', 'fsdp'), may hold values from -2 to 2
Outputs:
- master_out: float32 [2, 2048, 16384], P(None, 'replica', 'fsdp')
- momentum_out: float32 [2, 2048, 16384], P(None, 'replica', 'fsdp')
- params_out: bfloat16 [2, 2048, 16384], P(None, 'fsdp')
All inputs are finite; a program needn't handle non-finite values.
Results may differ from a plain program's by a relative error of at most 0.008.
Values may be sent and summed in bfloat16 or wider, within the bound.
A program may use at most 128 MiB of HBM per device.

v0:
```python
import jax
import jax.numpy as jnp
from jax import lax
from jax.sharding import PartitionSpec as P


def on_device(deltas, master, momentum):
    local = deltas[0]
    groups = lax.axis_size("replica")
    moved = lax.all_to_all(local, "fsdp", split_axis=2, concat_axis=1, tiled=True)
    summed = lax.psum_scatter(
        moved.astype(jnp.float32).astype(jnp.bfloat16), "replica", scatter_dimension=1, tiled=True
    ).astype(jnp.float32)
    outer = summed / groups
    velocity = 0.9 * momentum + outer
    updated = master - 0.7 * (outer + 0.9 * velocity)
    rounded = updated.astype(jnp.bfloat16)
    copies = lax.all_gather(rounded, "replica", axis=1, tiled=True)
    spread = lax.all_to_all(copies, "fsdp", split_axis=1, concat_axis=2, tiled=True)
    return (updated, velocity, spread)


def solution(mesh):
    return jax.shard_map(
        on_device,
        mesh=mesh,
        in_specs=(
            P("replica", None, "fsdp", None),
            P(None, "replica", "fsdp"),
            P(None, "replica", "fsdp"),
        ),
        out_specs=(P(None, "replica", "fsdp"), P(None, "replica", "fsdp"), P(None, "fsdp", None)),
        check_vma=False,
    )
```

profile of v0, /device:TPU:0, one launch (start us, length us, event | category | flops | bytes accessed | tf_op | source)
XLA Modules:
  0.0 1325.4 jit_solution(8873194051052167290)
XLA Ops:
  7.2 0.0 all-reduce.3.cloned.1.call-start
  7.2 40.8 %copy.22 = bf16[1,2,256,16384]{2,1,3,0:T(2,128)(2,1)} copy(bf16[1,2,256,16384]{3,2,1,0:T(8,128)(2,1)} %param.3) | data formatting | bytes 33554432 | tf_op args[0]
  48.0 372.0 %all_to_all.36 = bf16[2,256,16384]{1,0,2:T(2,128)(2,1)} all-to-all(bf16[2,256,16384]{1,0,2:T(2,128)(2,1)} %bitcast.14), channel_id=1, replica_groups=mesh['replica'=4,'fsdp'=8] {'fsdp'}, dimensions={2} | all-to-all | bytes 33554432 | tf_op jit(solution)/shard_map/all_to_all | solution.py:10
  420.0 60.3 %copy.23 = bf16[2,8,256,2048]{3,0,2,1:T(2,128)(2,1)} copy(bf16[2,8,256,2048]{2,0,3,1:T(2,128)(2,1)} %bitcast.12) | data formatting | bytes 33554432 | tf_op jit(solution)/shard_map/all_to_all | solution.py:10
  480.3 0.0 copy-start
  480.3 0.0 all-reduce.3.cloned.1.call-update
  480.3 0.0 all-gather.2.cloned.1.call-start
  480.4 0.6 copy-done
  481.0 0.6 dynamic-slice
  482.2 285.7 %all-reduce.3.cloned.1.call-done = bf16[2,2048,2048]{2,0,1:T(2,128)(2,1)} async-done(((bf16[2,2048,2048]{2,0,1:T(2,128)(2,1)}), bf16[2,2048,2048]{2,0,1:T(2,128)(2,1)}) %all-reduce.3.cloned.1.call-update) | async-done | bytes 16777232
  767.9 5.1 constant_dynamic-slice_fusion
  773.0 13.9 %fusion = (bf16[2,512,2048]{2,1,0:T(8,128)(2,1)}, f32[2,512,2048]{2,1,0:T(8,128)}, f32[2,512,2048]{2,1,0:T(8,128)}) fusion(f32[2,512,2048]{2,1,0:T(8,128)} %param.4, bf16[2,512,2048]{2,0,1:T(2,128)(2,1)S(1)} %constant_dynamic-slice_fusion, f32[2,512,2048]{2,1,0:T(8,128)} %param.5), kind=kLoop, calls=%fused_computation.4 | loop fusion | flops 18874368 | bytes 41943040 | tf_op jit(solution)/shard_map/convert_element_type | solution.py:17
  786.9 8.4 copy.25
  795.3 0.0 all-gather.2.cloned.1.call-update
  795.3 106.1 %all-gather.2.cloned.1.call-done = bf16[2,2048,2048]{2,0,1:T(2,128)(2,1)} async-done(((bf16[2,512,2048]{2,0,1:T(2,128)(2,1)}), bf16[2,2048,2048]{2,0,1:T(2,128)(2,1)}) %all-gather.2.cloned.1.call-update) | async-done | bytes 16777232 | tf_op jit(solution)/shard_map/all_gather | solution.py:18
  901.4 368.7 %all_to_all.37 = bf16[2,2048,2048]{2,0,1:T(2,128)(2,1)S(1)} all-to-all(bf16[2,2048,2048]{2,0,1:T(2,128)(2,1)} %all-gather.2.cloned.1.call-done), channel_id=1, replica_groups=mesh['replica'=4,'fsdp'=8] {'fsdp'}, dimensions={1} | all-to-all | bytes 33554432 | tf_op jit(solution)/shard_map/all_to_all | solution.py:19
  1270.1 22.9 %copy.26 = bf16[2,256,8,2048]{3,2,1,0:T(8,128)(2,1)} copy(bf16[2,256,8,2048]{3,0,1,2:T(2,128)(2,1)S(1)} %bitcast.13) | data formatting | bytes 33554432 | tf_op jit(solution)/shard_map/all_to_all | solution.py:19
  1293.0 25.5 %all_to_all.33 = bf16[2,256,16384]{2,1,0:T(8,128)(2,1)} reshape(bf16[2,256,8,2048]{3,2,1,0:T(8,128)(2,1)} %copy.26) | data formatting | bytes 33554432 | tf_op jit(solution)/shard_map/all_to_all | solution.py:19
Async XLA Ops:
  7.2 760.7 %all-reduce.3.cloned.1.call-start = ((), (), s32[]{:S(2)}) async-start(), calls=%async_computation.3 | async-start | bytes 33554432
  480.3 0.7 copy-start
  480.3 421.1 %all-gather.2.cloned.1.call-start = ((), (), s32[]{:S(2)}) async-start(), calls=%async_computation.2 | async-start | bytes 20971520 | tf_op jit(solution)/shard_map/all_gather | solution.py:18
Sparse Core Ops, SparseCore 0:
  480.4 287.3 all-reduce.2
  795.5 105.9 all-gather.1
where the time goes:
time: 1330 us
  blocking collectives  741 us (56%)
  waiting for transfers between devices  392 us (29%)
  local copies, waits for them, and re-layouts  164 us (12%)
  between operations  14.7 us (1%)
  other arithmetic  13.9 us (1%)
    all_to_all x1, blocking collectives, on_device(): lax.all_to_all(local, 'fsdp', split_axis=2, concat_axis=1, tiled=True)  372 us
    all_to_all x1, blocking collectives, on_device(): lax.all_to_all(copies, 'fsdp', split_axis=1, concat_axis=2, tiled=True)  369 us
    unnamed x3, waiting for transfers between devices  286 us
    all_gather x1, waiting for transfers between devices, on_device(): copies = lax.all_gather(rounded, 'replica', axis=1, tiled=True)  106 us
    all_to_all x1, local copies, waits for them, and re-layouts, on_device(): lax.all_to_all(local, 'fsdp', split_axis=2, concat_axis=1, tiled=True)  60.3 us
    all_to_all x2, local copies, waits for them, and re-layouts, on_device(): lax.all_to_all(copies, 'fsdp', split_axis=1, concat_axis=2, tiled=True)  48.4 us
    unnamed x5, local copies, waits for them, and re-layouts  47 us
  transfers between devices with their start and end apart: 2, of which 2 were waited for; matrix products, arithmetic and copies ran while one was open for 0% of the time, Pallas kernels for 0%

commit v1 on v0

--- a/solution.py
+++ b/solution.py
@@ -5,6 +5,10 @@
 
 
 def on_device(deltas, master, momentum):
+
+    def feed_views(mat, dim_k):
+        return jnp.concatenate(lax.all_gather(mat, "replica"), axis=dim_k)
+
     local = deltas[0]
     groups = lax.axis_size("replica")
     moved = lax.all_to_all(local, "fsdp", split_axis=2, concat_axis=1, tiled=True)
@@ -15,7 +19,7 @@
     velocity = 0.9 * momentum + outer
     updated = master - 0.7 * (outer + 0.9 * velocity)
     rounded = updated.astype(jnp.bfloat16)
-    copies = lax.all_gather(rounded, "replica", axis=1, tiled=True)
+    copies = feed_views(rounded, 1)
     spread = lax.all_to_all(copies, "fsdp", split_axis=1, concat_axis=2, tiled=True)
     return (updated, velocity, spread)
 

time: 1330 us -> 1200 us (0.902)
  waiting for transfers between devices: 392 us -> 230 us
  local copies, waits for them, and re-layouts: 164 us -> 195 us
    unnamed x3 -> x2, waiting for transfers between devices: 286 us -> 0.03 us
    reduce_scatter x0 -> x1, waiting for transfers between devices: none -> 124 us  [on_device(): lax.psum_scatter(moved.astype(jnp.float32).astype(jnp.bfloat16), 'replica...]
    reshape x0 -> x2, local copies, waits for them, and re-layouts: none -> 57.4 us  [feed_views(): return jnp.concatenate(lax.all_gather(mat, 'replica'), axis=dim_k)]
    all_to_all x1, local copies, waits for them, and re-layouts: 60.3 us -> 40.8 us  [on_device(): lax.all_to_all(local, 'fsdp', split_axis=2, concat_axis=1, tiled=True)]
    unnamed x5 -> x2, local copies, waits for them, and re-layouts: 47 us -> 61.9 us
    all_to_all x2, local copies, waits for them, and re-layouts: 48.4 us -> 34.9 us  [on_device(): lax.all_to_all(copies, 'fsdp', split_axis=1, concat_axis=2, tiled=True)]
where the time goes in v1:
time: 1200 us; the launch traced here: 1190 us
  blocking collectives  741 us (62%)
  waiting for transfers between devices  230 us (19%)
  local copies, waits for them, and re-layouts  195 us (16%)
  between operations  14 us (1%)
  other arithmetic  13.3 us (1%)
    all_to_all x1, blocking collectives, on_device(): lax.all_to_all(local, 'fsdp', split_axis=2, concat_axis=1, tiled=True)  372 us
    all_to_all x1, blocking collectives, on_device(): lax.all_to_all(copies, 'fsdp', split_axis=1, concat_axis=2, tiled=True)  369 us
    reduce_scatter x1, waiting for transfers between devices, on_device(): lax.psum_scatter(moved.astype(jnp.float32).astype(jnp.bfloat16), 'replica...  124 us
    all_gather x1, waiting for transfers between devices, feed_views(): return jnp.concatenate(lax.all_gather(mat, 'replica'), axis=dim_k)  106 us
    unnamed x2, local copies, waits for them, and re-layouts  61.9 us
    reshape x2, local copies, waits for them, and re-layouts, feed_views(): return jnp.concatenate(lax.all_gather(mat, 'replica'), axis=dim_k)  57.4 us
    all_to_all x1, local copies, waits for them, and re-layouts, on_device(): lax.all_to_all(local, 'fsdp', split_axis=2, concat_axis=1, tiled=True)  40.8 us
    all_to_all x2, local copies, waits for them, and re-layouts, on_device(): lax.all_to_all(copies, 'fsdp', split_axis=1, concat_axis=2, tiled=True)  34.9 us
  transfers between devices with their start and end apart: 2, of which 2 were waited for; matrix products, arithmetic and copies ran while one was open for 0% of the time, Pallas kernels for 0%

profile of v1, /device:TPU:0, one launch (start us, length us, event | category | flops | bytes accessed | tf_op | source)
XLA Modules:
  0.0 1193.4 jit_solution(3925367726308313737)
XLA Ops:
  7.2 0.0 reduce-scatter.2.cloned.1.call-start
  7.2 40.8 %copy.12 = bf16[1,2,256,16384]{2,1,3,0:T(2,128)(2,1)} copy(bf16[1,2,256,16384]{3,2,1,0:T(8,128)(2,1)} %param.3) | data formatting | bytes 33554432 | tf_op args[0]
  48.0 372.0 %all_to_all.36 = bf16[2,256,16384]{1,0,2:T(2,128)(2,1)} all-to-all(bf16[2,256,16384]{1,0,2:T(2,128)(2,1)} %bitcast.18), channel_id=1, replica_groups=mesh['replica'=4,'fsdp'=8] {'fsdp'}, dimensions={2} | all-to-all | bytes 33554432 | tf_op jit(solution)/shard_map/all_to_all | solution.py:14
  420.0 40.8 %copy.13 = bf16[2,8,256,2048]{3,2,1,0:T(8,128)(2,1)} copy(bf16[2,8,256,2048]{2,0,3,1:T(2,128)(2,1)} %bitcast.14) | data formatting | bytes 33554432 | tf_op jit(solution)/shard_map/all_to_all | solution.py:14
  460.8 0.0 reduce-scatter.2.cloned.1.call-update
  460.8 0.0 all-gather.3.cloned.1.call-start
  460.9 124.2 %reduce-scatter.2.cloned.1.call-done = bf16[2,512,2048]{2,1,0:T(8,128)(2,1)} async-done(((bf16[2,2048,2048]{2,1,0:T(8,128)(2,1)}), bf16[2,512,2048]{2,1,0:T(8,128)(2,1)}) %reduce-scatter.2.cloned.1.call-update) | async-done | bytes 4194320 | tf_op jit(solution)/shard_map/reduce_scatter | solution.py:15
  585.0 13.3 %fusion = (bf16[2,512,2048]{2,1,0:T(8,128)(2,1)}, f32[2,512,2048]{2,1,0:T(8,128)}, f32[2,512,2048]{2,1,0:T(8,128)}) fusion(f32[2,512,2048]{2,1,0:T(8,128)} %param.4, bf16[2,512,2048]{2,1,0:T(8,128)(2,1)} %reduce-scatter.2.cloned.1.call-done, f32[2,512,2048]{2,1,0:T(8,128)} %param.5), kind=kLoop, calls=%fused_computation.3 | loop fusion | flops 18874368 | bytes 41943040 | tf_op jit(solution)/shard_map/convert_element_type | solution.py:21
  598.3 0.0 all-gather.3.cloned.1.call-update
  598.3 106.0 %all-gather.3.cloned.1.call-done = bf16[8,512,2048]{2,1,0:T(8,128)(2,1)} async-done(((bf16[2,512,2048]{2,1,0:T(8,128)(2,1)}), bf16[8,512,2048]{2,1,0:T(8,128)(2,1)}) %all-gather.3.cloned.1.call-update) | async-done | bytes 16777232 | tf_op jit(solution)/shard_map/all_gather | solution.py:10
  704.4 8.5 copy.14
  712.9 48.9 %copy.15 = bf16[2,2048,2048]{2,0,1:T(2,128)(2,1)} copy(bf16[2,2048,2048]{2,1,0:T(8,128)(2,1)S(1)} %bitcast.15) | data formatting | bytes 33554432 | tf_op jit(solution)/shard_map/reshape | solution.py:10
  761.8 368.7 %all_to_all.37 = bf16[2,2048,2048]{2,0,1:T(2,128)(2,1)S(1)} all-to-all(bf16[2,2048,2048]{2,0,1:T(2,128)(2,1)} %copy.15), channel_id=1, replica_groups=mesh['replica'=4,'fsdp'=8] {'fsdp'}, dimensions={1} | all-to-all | bytes 33554432 | tf_op jit(solution)/shard_map/all_to_all | solution.py:23
  1130.5 13.3 %copy.16 = bf16[2,2048,2048]{2,1,0:T(8,128)(2,1)} copy(bf16[2,2048,2048]{2,0,1:T(2,128)(2,1)S(1)} %all_to_all.37) | data formatting | bytes 33554432 | tf_op jit(solution)/shard_map/all_to_all | solution.py:23
  1143.8 21.5 %copy.17 = bf16[2,256,8,2048]{1,3,2,0:T(8,128)(2,1)} copy(bf16[2,256,8,2048]{3,1,2,0:T(8,128)(2,1)} %bitcast.16) | data formatting | bytes 33554432 | tf_op jit(solution)/shard_map/all_to_all | solution.py:23
  1165.3 21.2 %copy.18 = bf16[2,256,16384]{2,1,0:T(8,128)(2,1)} copy(bf16[2,256,16384]{1,2,0:T(8,128)(2,1)} %bitcast.17) | data formatting | bytes 33554432
Async XLA Ops:
  7.2 577.9 %reduce-scatter.2.cloned.1.call-start = ((), (), s32[]{:S(2)}) async-start(), calls=%async_computation.3 | async-start | bytes 20971520 | tf_op jit(solution)/shard_map/reduce_scatter | solution.py:15
  460.8 243.6 %all-gather.3.cloned.1.call-start = ((), (), s32[]{:S(2)}) async-start(), calls=%async_computation.4 | async-start | bytes 20971520 | tf_op jit(solution)/shard_map/all_gather | solution.py:10
Sparse Core Ops, SparseCore 0:
  460.9 124.0 reduce-scatter.1
  598.5 105.8 all-gather.2
